TPU v7x, 32 devices: a 4x4x1 block of a 4x4x8 slice. The times are simulated.
32 devices in a mesh: data: 1 (over z), fsdp: 32 (over y, x, core).
Axes of the slice: x: 4, y: 4, z: 1, core: 2. Of those that a mesh axis runs over, the one named last changes fastest.
The devices are a block of a 4x4x8 slice.
Arguments:
- hidden: bfloat16 [16384, 2048], P('data')
- targets: int32 [16384], P('data')
- w_out: bfloat16 [49152, 2048], P('fsdp')
Outputs:
- output 1: float32 [1], P('data')
- output 2: float32 [16384, 2048], P(('data', 'fsdp'))
- output 3: float32 [49152, 2048], P(('data', 'fsdp'))
All inputs are finite; a program needn't handle non-finite values.
Results may differ from a plain program's by a relative error of at most 0.001.
Values are sent between devices in bfloat16 or wider.
A program may use at most 768 MiB of HBM per device.

v0:
```python
import functools
import math

import jax
import jax.numpy as jnp
from jax import lax
from jax.experimental import pallas as pl
from jax.experimental.pallas import tpu as pltpu
from jax.sharding import PartitionSpec as P

F32 = jnp.float32
BF16 = jnp.bfloat16
LOG2E = 1.4426950408889634
LN2 = 0.6931471805599453
ROWS = 16
AXIS = "fsdp"

FAR1, PURE1, MERGED1, FAR2, PURE2, MERGED2 = range(6)


def dot_nt(a, b):
    return lax.dot_general(a, b, (((1,), (1,)), ((), ())), preferred_element_type=F32)


def dot_nn(a, b):
    return lax.dot_general(a, b, (((1,), (0,)), ((), ())), preferred_element_type=F32)


def dot_tn(a, b):
    return lax.dot_general(a, b, (((0,), (0,)), ((), ())), preferred_element_type=F32)


def join(parts):
    top = functools.reduce(jnp.maximum, parts)
    total = functools.reduce(jnp.add, [jnp.exp2(v - top) for v in parts])
    return top + jnp.log(total) * LOG2E


def head_kernel(
    group, side, chunks, tokens,
    hid, tgt, w_hbm,
    loss_ref, dh_hbm, dw_hbm,
    wb, dwacc, hb, yb, dz, dzr, sb, tb, far1, pure1, merged1, far2, pure2, merged2, ob,
    stat, own, st0, mid, st1, row, st2, lse, lossacc,
    wsem, hsem, rs_send, rs_recv, dz_send, dz_recv, w_send, w_recv,
    st0_send, st0_recv, st1_send, st1_recv, st2_send, st2_recv, osem, dwsem,
):
    vocab, dim = w_hbm.shape
    half = dim // 2
    mt = vocab // 2
    tok = hb.shape[1] * hb.shape[2] * ROWS
    tokc = tok // 2

    me = lax.axis_index(AXIS)
    core = lax.rem(me, 2)
    other = 1 - core
    x = lax.rem(me // 2, side)
    y = me // (2 * side)
    p = x + core * (y - x)
    q = y + core * (x - y)
    partner = me + 1 - 2 * core

    def at_xy(xx, yy):
        return (lax.rem(yy + side, side) * side + lax.rem(xx + side, side)) * 2 + core

    def at_pq(pp, qq):
        return at_xy(pp + core * (qq - pp), qq + core * (pp - qq))

    peers_x = [at_xy(x + k, y) for k in range(1, side)]
    peers_y = [at_xy(x, y + k) for k in range(1, side)]
    to_p, to_q = (at_pq(p + 1, q), at_pq(p - 1, q)), (at_pq(p, q + 1), at_pq(p, q - 1))
    near_p = lax.rem(p + 1, side), lax.rem(p + side - 1, side), lax.rem(p + 2, side)
    near_q = lax.rem(q + 1, side), lax.rem(q + side - 1, side), lax.rem(q + 2, side)

    def rcopy(src, dst, send, recv, dev):
        return pltpu.make_async_remote_copy(
            src_ref=src, dst_ref=dst, send_sem=send, recv_sem=recv,
            device_id={AXIS: dev}, device_id_type=pl.DeviceIdType.MESH,
        )

    def guarded(cond, fn):
        pl.when(cond)(fn)

    barrier = pltpu.get_barrier_semaphore()
    friends = [partner, *peers_x, *peers_y]
    for dev in friends:
        pl.semaphore_signal(barrier, inc=1, device_id={AXIS: dev}, device_id_type=pl.DeviceIdType.MESH)

    def h_copies(c):
        s = lax.rem(c, 4)
        out = []
        for k in range(side):
            out.append(pltpu.make_async_copy(hid.at[:, k, 0, c], hb.at[s, k], hsem.at[s]))
            out.append(pltpu.make_async_copy(hid.at[k, :, 1, c], hb.at[s, side + k], hsem.at[s]))
        return out

    def h_start(c):
        for d in h_copies(c):
            d.start()

    def h_wait(c):
        s = lax.rem(c, 4)
        pltpu.make_async_copy(hb.at[s], hb.at[s], hsem.at[s]).wait()

    w_local = pltpu.make_async_copy(w_hbm, wb.at[core], wsem)
    w_local.start()
    h_start(0)
    dwacc[...] = jnp.zeros_like(dwacc)
    lossacc[...] = jnp.zeros_like(lossacc)
    pl.semaphore_wait(barrier, len(friends))
    w_local.wait()
    w_remote = rcopy(wb.at[core], wb.at[core], w_send, w_recv, partner)
    w_remote.start()

    def rs(kind, c):
        s = lax.rem(c, 2)
        lo, hi = pl.ds(0, half), pl.ds(half, half)
        buf, to, (up, down, far) = (sb, to_p, near_p) if kind < 3 else (tb, to_q, near_q)
        dst = (far1, pure1, merged1, far2, pure2, merged2)[kind]
        src = {0: ((far, lo), (far, hi)), 1: ((up, hi), (down, lo)), 2: ((up, lo), (down, hi))}[kind % 3]
        return [
            rcopy(buf.at[s, src[d][0], :, src[d][1]], dst.at[s, d], rs_send.at[kind, s, d], rs_recv.at[kind, s, d], to[d])
            for d in range(2)
        ]

    def start(ds):
        for d in ds:
            d.start()

    def wait_recv(ds):
        for d in ds:
            d.wait_recv()

    def wait_send(ds):
        for d in ds:
            d.wait_send()

    def dz_copy(c):
        s = lax.rem(c, 2)
        return [rcopy(dz.at[other], dzr.at[s], dz_send, dz_recv.at[s], partner)]

    def st0_copy(i):
        s = lax.rem(i, 2)
        return [rcopy(own.at[s], st0.at[s], st0_send.at[s], st0_recv.at[s], partner)]

    def st1_copy(i):
        s = lax.rem(i, 2)
        return [
            rcopy(mid.at[s], st1.at[s, x], st1_send.at[s, k], st1_recv.at[s, k], peer)
            for k, peer in enumerate(peers_x)
        ]

    def st2_copy(i):
        s = lax.rem(i, 2)
        return [
            rcopy(row.at[s], st2.at[s, y], st2_send.at[s, k], st2_recv.at[s, k], peer)
            for k, peer in enumerate(peers_y)
        ]

    def two(fn):
        lax.fori_loop(0, 2, lambda j, carry: (fn(j), carry)[1], 0)

    def logits(i, j, slot):
        r = pl.ds(pl.multiple_of(j * mt, mt), mt)
        h = hb[lax.rem(i, 4)].reshape(tok, dim)
        yb[slot, r, :] = dot_nt(wb[core, r, :], h) * LOG2E

    def grad_logits(c, j, slot):
        r = pl.ds(pl.multiple_of(j * mt, mt), mt)
        prob = jnp.exp2(yb[slot, r, :] - lse[0:1, :])
        hit = lax.broadcasted_iota(jnp.int32, prob.shape, 0) == tgt[c] - (me * vocab + j * mt)
        g = (prob + jnp.where(hit, -1.0 / tokens, 0.0)).astype(BF16)
        dz[0, r, :] = g[:, :tokc]
        dz[1, r, :] = g[:, tokc:]

    def statistics(i, j, slot):
        v = yb[slot, pl.ds(pl.multiple_of(j * mt, mt), mt), :]
        top = jnp.max(v, axis=0, keepdims=True)
        total = jnp.sum(jnp.exp2(v - top), axis=0, keepdims=True)
        hit = lax.broadcasted_iota(jnp.int32, v.shape, 0) == tgt[lax.rem(i, chunks)] - (me * vocab + j * mt)
        stat[j, 0:1, :] = top + jnp.log(total) * LOG2E
        stat[j, 1:2, :] = jnp.sum(jnp.where(hit, v, 0.0), axis=0, keepdims=True)

    def grad_w(c, k):
        n = dim // 2
        cols = pl.ds(pl.multiple_of(k * n, n), n)
        h = hb[lax.rem(c, 4), :, :, :, cols].reshape(tok, n)
        dwacc[:, cols] += dot_nn(dz[0], h[:tokc]) + dot_nn(dz[1], h[tokc:])

    def grad_h(c):
        s = lax.rem(c, 2)
        v = dot_tn(dz[core], wb[core]) + dot_tn(dzr[s], wb[other])
        sb[s] = v.reshape(side, side * ROWS, dim)

    def finish(c):
        s = lax.rem(c, 2)
        wait_recv(rs(PURE2, c) + rs(MERGED2, c))
        wait_send(rs(FAR2, c) + rs(PURE2, c) + rs(MERGED2, c))
        guarded(c >= 2, lambda: pltpu.make_async_copy(ob.at[s], dh_hbm.at[c - 2], osem.at[s]).wait())
        ob[s, :, :half] = tb[s, q, :, :half] + merged2[s, 0] + pure2[s, 1]
        ob[s, :, half:] = tb[s, q, :, half:] + pure2[s, 0] + merged2[s, 1]
        pltpu.make_async_copy(ob.at[s], dh_hbm.at[c], osem.at[s]).start()

    def turn(c):
        s = lax.rem(c, 2)
        wait_recv(rs(PURE1, c) + rs(MERGED1, c))
        lo = sb[s, p, :, :half] + merged1[s, 0] + pure1[s, 1]
        hi = sb[s, p, :, half:] + pure1[s, 0] + merged1[s, 1]
        tb[s, :, :, :half] = lo.reshape(side, ROWS, half)
        tb[s, :, :, half:] = hi.reshape(side, ROWS, half)
        start(rs(FAR2, c) + rs(PURE2, c))
        wait_send(rs(FAR1, c) + rs(PURE1, c) + rs(MERGED1, c))

    def merge1(c):
        s = lax.rem(c, 2)
        up, down, _ = near_p
        wait_recv(rs(FAR1, c))
        sb[s, up, :, :half] += far1[s, 0]
        sb[s, down, :, half:] += far1[s, 1]
        start(rs(MERGED1, c))

    def merge2(c):
        s = lax.rem(c, 2)
        up, down, _ = near_q
        wait_recv(rs(FAR2, c))
        tb[s, up, :, :half] += far2[s, 0]
        tb[s, down, :, half:] += far2[s, 1]
        start(rs(MERGED2, c))

    def st_own(i):
        s = lax.rem(i, 2)
        guarded(i >= 2, lambda: wait_send(st0_copy(i)))
        own[s, 0:1, :] = join([stat[0, 0:1, :], stat[1, 0:1, :]])
        own[s, 1:2, :] = stat[0, 1:2, :] + stat[1, 1:2, :]
        start(st0_copy(i))

    def st_pair(i):
        s = lax.rem(i, 2)
        wait_recv(st0_copy(i))
        guarded(i >= 2, lambda: wait_send(st1_copy(i)))
        mid[s, 0:1, :] = join([own[s, 0:1, :], st0[s, 0:1, :]])
        mid[s, 1:2, :] = own[s, 1:2, :] + st0[s, 1:2, :]
        st1[s, x] = mid[s]
        start(st1_copy(i))

    def st_row(i):
        s = lax.rem(i, 2)
        wait_recv(st1_copy(i))
        guarded(i >= 2, lambda: wait_send(st2_copy(i)))
        row[s, 0:1, :] = join([st1[s, k, 0:1, :] for k in range(side)])
        row[s, 1:2, :] = functools.reduce(jnp.add, [st1[s, k, 1:2, :] for k in range(side)])
        st2[s, y] = row[s]
        start(st2_copy(i))

    def st_all(i):
        s = lax.rem(i, 2)
        wait_recv(st2_copy(i))
        full = join([st2[s, k, 0:1, :] for k in range(side)])
        hit = functools.reduce(jnp.add, [st2[s, k, 1:2, :] for k in range(side)])
        lse[0:1, :] = full + math.log2(tokens)
        lossacc[...] += full - hit

    def step(i, carry):
        c = i - 2
        slot = lax.rem(i, 2)
        has_a, has_c = i < chunks, jnp.logical_and(c >= 0, c < chunks)

        @pl.when(i + 1 < chunks)
        def _():
            h_start(i + 1)

        @pl.when(has_a)
        def _():
            h_wait(i)

        @pl.when(jnp.logical_and(has_a, has_c))
        def _():
            two(lambda j: (grad_logits(c, j, slot), logits(i, j, slot)))

        @pl.when(jnp.logical_and(has_a, jnp.logical_not(has_c)))
        def _():
            two(lambda j: logits(i, j, slot))
            two(lambda j: statistics(i, j, slot))

        @pl.when(jnp.logical_and(has_c, jnp.logical_not(has_a)))
        def _():
            two(lambda j: grad_logits(c, j, slot))

        def live(k):
            return jnp.logical_and(k >= 0, k < chunks)

        @pl.when(has_c)
        def _():
            start(dz_copy(c))

        guarded(live(c - 3), lambda: finish(c - 3))
        guarded(live(c - 2), lambda: turn(c - 2))
        guarded(live(c - 1), lambda: start(rs(PURE1, c - 1)))
        guarded(live(i - 1), lambda: st_row(i - 1))

        @pl.when(has_c)
        def _():
            two(lambda j: (statistics(i, j, slot), grad_w(c, j)))

        guarded(live(c - 1), lambda: merge1(c - 1))
        guarded(live(c - 2), lambda: merge2(c - 2))
        guarded(has_a, lambda: st_own(i))

        @pl.when(has_c)
        def _():
            guarded(c == 0, w_remote.wait_recv)
            wait_recv(dz_copy(c))
            grad_h(c)

        guarded(has_a, lambda: st_pair(i))

        @pl.when(has_c)
        def _():
            start(rs(FAR1, c))
            wait_send(dz_copy(c))

        guarded(live(i - 1), lambda: st_all(i - 1))

        @pl.when(c == chunks - 1)
        def _():
            pltpu.make_async_copy(dwacc, dw_hbm, dwsem).start()

        return carry

    lax.fori_loop(0, chunks + 5, step, 0)

    for i in range(max(chunks - 2, 0), chunks):
        wait_send(st0_copy(i) + st1_copy(i) + st2_copy(i))
        pltpu.make_async_copy(ob.at[i % 2], dh_hbm.at[i], osem.at[i % 2]).wait()
    w_remote.wait_send()
    pltpu.make_async_copy(dwacc, dw_hbm, dwsem).wait()
    loss_ref[...] = jnp.broadcast_to(jnp.sum(lossacc[...], axis=1, keepdims=True) * (LN2 / tokens), loss_ref.shape)


def solution(mesh):
    group = mesh.shape[AXIS]
    side = math.isqrt(group // 2)

    def local_step(hidden, targets, w_blk):
        tokens, dim = hidden.shape
        vocab = w_blk.shape[0]
        chunks = tokens // group // ROWS
        tok = group * ROWS
        half = dim // 2
        hid = hidden.reshape(side, side, 2, chunks, ROWS, dim)
        t = targets.reshape(side, side, 2, chunks, ROWS)
        tgt = jnp.concatenate(
            [t[:, :, 0].transpose(2, 1, 0, 3).reshape(chunks, 1, tok // 2), t[:, :, 1].transpose(2, 0, 1, 3).reshape(chunks, 1, tok // 2)],
            axis=2,
        )
        dma = pltpu.SemaphoreType.DMA
        any_spec = pl.BlockSpec(memory_space=pl.ANY)
        vmem_spec = pl.BlockSpec(memory_space=pltpu.VMEM)
        big, small = (2, 2, side * ROWS, half), (2, 2, ROWS, half)
        loss, dh, dw = pl.pallas_call(
            functools.partial(head_kernel, group, side, chunks, tokens),
            out_shape=(
                jax.ShapeDtypeStruct((1, 128), F32),
                jax.ShapeDtypeStruct((chunks, ROWS, dim), F32),
                jax.ShapeDtypeStruct((vocab, dim), F32),
            ),
            in_specs=[any_spec, vmem_spec, any_spec],
            out_specs=(vmem_spec, any_spec, any_spec),
            scratch_shapes=[
                pltpu.VMEM((2, vocab, dim), BF16),
                pltpu.VMEM((vocab, dim), F32),
                pltpu.VMEM((4, 2 * side, side, ROWS, dim), BF16),
                pltpu.VMEM((2, vocab, tok), F32),
                pltpu.VMEM((2, vocab, tok // 2), BF16),
                pltpu.VMEM((2, vocab, tok // 2), BF16),
                pltpu.VMEM((2, side, side * ROWS, dim), F32),
                pltpu.VMEM((2, side, ROWS, dim), F32),
                *[pltpu.VMEM(big, F32)] * 3,
                *[pltpu.VMEM(small, F32)] * 3,
                pltpu.VMEM((2, ROWS, dim), F32),
                pltpu.VMEM((2, 2, tok), F32),
                pltpu.VMEM((2, 2, tok), F32),
                pltpu.VMEM((2, 2, tok), F32),
                pltpu.VMEM((2, 2, tok), F32),
                pltpu.VMEM((2, side, 2, tok), F32),
                pltpu.VMEM((2, 2, tok), F32),
                pltpu.VMEM((2, side, 2, tok), F32),
                pltpu.VMEM((1, tok), F32),
                pltpu.VMEM((1, tok), F32),
                dma, dma((4,)),
                dma((6, 2, 2)), dma((6, 2, 2)),
                dma, dma((2,)), dma, dma,
                dma((2,)), dma((2,)),
                dma((2, side - 1)), dma((2, side - 1)),
                dma((2, side - 1)), dma((2, side - 1)),
                dma((2,)), dma,
            ],
            compiler_params=pltpu.CompilerParams(
                collective_id=0, has_side_effects=True, vmem_limit_bytes=67043328,
            ),
            name="head",
        )(hid, tgt, w_blk)
        return loss[0, :1], dh.reshape(tokens // group, dim), dw

    return jax.shard_map(
        local_step,
        mesh=mesh,
        in_specs=(P("data", None), P("data"), P(AXIS, None)),
        out_specs=(P("data"), P(("data", AXIS), None), P(("data", AXIS), None)),
        check_vma=False,
    )
```

profile of v0, /device:TPU:96, one launch (start us, length us, event | category | flops | bytes accessed | tf_op | source)
XLA Modules:
  0.0 447.8 jit_solution(1598825084292968925)
XLA Ops:
  0.6 1.0 reshape.22
  1.7 0.1 copy.7
  1.8 0.1 copy.9
  1.9 0.1 copy.8
  2.0 0.1 copy.10
  2.1 0.7 pad_add_fusion.tgt
  2.8 427.1 %head.1 = (f32[1,128]{1,0:T(1,128)}, f32[32,16,2048]{2,1,0:T(8,128)}, f32[1536,2048]{1,0:T(8,128)}) custom-call(bf16[4,4,2,32,16,2048]{5,4,3,2,1,0:T(8,128)(2,1)} %bitcast.hid, s32[32,1,512]{2,1,0:T(1,128)} %pad_add_fusion.tgt, bf16[1536,2048]{1,0:T(8,128)(2,1)} %w_hbm.1), custom_call_target="tpu_custom_call" | custom-call | tf_op jit(solution)/shard_map/head/pallas_call | solution.py:360
  430.5 4.7 %copy.15 = f32[512,2048]{1,0:T(8,128)} copy(f32[512,2048]{1,0:T(8,128)} %bitcast.14) | data formatting | bytes 8388608
  435.2 11.5 %copy.16 = f32[1536,2048]{1,0:T(8,128)} copy(f32[1536,2048]{1,0:T(8,128)} %get-tuple-element.16) | data formatting | bytes 25165824
  (1 shorter events, 0.0 us)
where the time goes:
time: 448 us
  Pallas kernels  427 us (95%)
  local copies, waits for them, and re-layouts  17.7 us (4%)
    pallas_call x1, Pallas kernels, local_step(): pl.pallas_call(functools.partial(head_kernel, group, side, chunks, tokens...  427 us
    unnamed x2, local copies, waits for them, and re-layouts  16.2 us

commit v1 on v0

--- a/solution.py
+++ b/solution.py
@@ -12,6 +12,7 @@
 BF16 = jnp.bfloat16
 LOG2E = 1.4426950408889634
 LN2 = 0.6931471805599453
+LATER = 3
 ROWS = 16
 AXIS = "fsdp"
 
@@ -39,15 +40,16 @@
 def head_kernel(
     group, side, chunks, tokens,
     hid, tgt, w_hbm,
-    loss_ref, dh_hbm, dw_hbm,
+    loss_ref, dh_hbm, dw_hbm, dz_hbm,
     wb, dwacc, hb, yb, dz, dzr, sb, tb, far1, pure1, merged1, far2, pure2, merged2, ob,
     stat, own, st0, mid, st1, row, st2, lse, lossacc,
     wsem, hsem, rs_send, rs_recv, dz_send, dz_recv, w_send, w_recv,
-    st0_send, st0_recv, st1_send, st1_recv, st2_send, st2_recv, osem, dwsem,
+    st0_send, st0_recv, st1_send, st1_recv, st2_send, st2_recv, osem, dwsem, dxsem,
 ):
     vocab, dim = w_hbm.shape
     half = dim // 2
     mt = vocab // 2
+    stride = chunks // (LATER + 1)
     tok = hb.shape[1] * hb.shape[2] * ROWS
     tokc = tok // 2
 
@@ -59,6 +61,7 @@
     p = x + core * (y - x)
     q = y + core * (x - y)
     partner = me + 1 - 2 * core
+    one = 1 + me // group
 
     def at_xy(xx, yy):
         return (lax.rem(yy + side, side) * side + lax.rem(xx + side, side)) * 2 + core
@@ -137,7 +140,7 @@
 
     def dz_copy(c):
         s = lax.rem(c, 2)
-        return [rcopy(dz.at[other], dzr.at[s], dz_send, dz_recv.at[s], partner)]
+        return [rcopy(dz.at[s, other], dzr.at[s], dz_send, dz_recv.at[s], partner)]
 
     def st0_copy(i):
         s = lax.rem(i, 2)
@@ -170,8 +173,8 @@
         prob = jnp.exp2(yb[slot, r, :] - lse[0:1, :])
         hit = lax.broadcasted_iota(jnp.int32, prob.shape, 0) == tgt[c] - (me * vocab + j * mt)
         g = (prob + jnp.where(hit, -1.0 / tokens, 0.0)).astype(BF16)
-        dz[0, r, :] = g[:, :tokc]
-        dz[1, r, :] = g[:, tokc:]
+        dz[slot, 0, r, :] = g[:, :tokc]
+        dz[slot, 1, r, :] = g[:, tokc:]
 
     def statistics(i, j, slot):
         v = yb[slot, pl.ds(pl.multiple_of(j * mt, mt), mt), :]
@@ -185,11 +188,12 @@
         n = dim // 2
         cols = pl.ds(pl.multiple_of(k * n, n), n)
         h = hb[lax.rem(c, 4), :, :, :, cols].reshape(tok, n)
-        dwacc[:, cols] += dot_nn(dz[0], h[:tokc]) + dot_nn(dz[1], h[tokc:])
+        s = lax.rem(c, 2)
+        dwacc[:, cols] += dot_nn(dz[s, 0], h[:tokc]) + dot_nn(dz[s, 1], h[tokc:])
 
     def grad_h(c):
         s = lax.rem(c, 2)
-        v = dot_tn(dz[core], wb[core]) + dot_tn(dzr[s], wb[other])
+        v = dot_tn(dz[s, core], wb[core]) + dot_tn(dzr[s], wb[other])
         sb[s] = v.reshape(side, side * ROWS, dim)
 
     def finish(c):
@@ -296,11 +300,32 @@
         guarded(live(c - 3), lambda: finish(c - 3))
         guarded(live(c - 2), lambda: turn(c - 2))
         guarded(live(c - 1), lambda: start(rs(PURE1, c - 1)))
-        guarded(live(i - 1), lambda: st_row(i - 1))
-
-        @pl.when(has_c)
-        def _():
-            two(lambda j: (statistics(i, j, slot), grad_w(c, j)))
+        later = jnp.logical_and(lax.rem(c, stride) == stride - 1, c // stride < LATER)
+        now = jnp.logical_and(jnp.logical_and(c >= 0, c < chunks - 2), jnp.logical_not(later))
+        save = jnp.logical_and(jnp.logical_and(c >= 0, c < chunks - 2), later)
+
+        @pl.when(now)
+        def _():
+            def half_dw(j):
+                statistics(i, j, slot)
+                grad_w(c, j)
+
+            lax.fori_loop(0, one, lambda j, u: (half_dw(j), u)[1], 0)
+            guarded(live(i - 1), lambda: st_row(i - 1))
+            lax.fori_loop(one, 2, lambda j, u: (half_dw(j), u)[1], 0)
+
+        @pl.when(jnp.logical_not(now))
+        def _():
+            @pl.when(save)
+            def _():
+                pltpu.make_async_copy(dz.at[lax.rem(c + 2, 2)], dz_hbm.at[c // stride], dxsem).start()
+                two(lambda j: statistics(i, j, slot))
+
+            guarded(live(i - 1), lambda: st_row(i - 1))
+
+        @pl.when(c == chunks)
+        def _():
+            two(lambda j: grad_w(c - 2, j))
 
         guarded(live(c - 1), lambda: merge1(c - 1))
         guarded(live(c - 2), lambda: merge2(c - 2))
@@ -319,10 +344,15 @@
             start(rs(FAR1, c))
             wait_send(dz_copy(c))
 
+        @pl.when(save)
+        def _():
+            pltpu.make_async_copy(dz.at[lax.rem(c + 2, 2)], dz_hbm.at[c // stride], dxsem).wait()
+
         guarded(live(i - 1), lambda: st_all(i - 1))
 
-        @pl.when(c == chunks - 1)
-        def _():
+        @pl.when(c == chunks)
+        def _():
+            two(lambda j: grad_w(c - 1, j))
             pltpu.make_async_copy(dwacc, dw_hbm, dwsem).start()
 
         return carry
@@ -335,6 +365,18 @@
     w_remote.wait_send()
     pltpu.make_async_copy(dwacc, dw_hbm, dwsem).wait()
     loss_ref[...] = jnp.broadcast_to(jnp.sum(lossacc[...], axis=1, keepdims=True) * (LN2 / tokens), loss_ref.shape)
+
+
+def last_kernel(side, dw_ref, dh_ref, dz_ref, *rest):
+    hid, (dw_out, dh_out) = rest[:LATER], rest[LATER:]
+    total = dw_ref[...]
+    for k in range(LATER):
+        h = hid[k]
+        by_x = [h[yy, xx, 0, 0] for xx in range(side) for yy in range(side)]
+        by_y = [h[yy, xx, 1, 0] for yy in range(side) for xx in range(side)]
+        total += dot_nn(dz_ref[k, 0], jnp.concatenate(by_x, axis=0)) + dot_nn(dz_ref[k, 1], jnp.concatenate(by_y, axis=0))
+    dw_out[...] = total
+    dh_out[...] = dh_ref[...]
 
 
 def solution(mesh):
@@ -357,21 +399,22 @@
         any_spec = pl.BlockSpec(memory_space=pl.ANY)
         vmem_spec = pl.BlockSpec(memory_space=pltpu.VMEM)
         big, small = (2, 2, side * ROWS, half), (2, 2, ROWS, half)
-        loss, dh, dw = pl.pallas_call(
+        loss, dh, dw, dz_left = pl.pallas_call(
             functools.partial(head_kernel, group, side, chunks, tokens),
             out_shape=(
                 jax.ShapeDtypeStruct((1, 128), F32),
                 jax.ShapeDtypeStruct((chunks, ROWS, dim), F32),
                 jax.ShapeDtypeStruct((vocab, dim), F32),
+                jax.ShapeDtypeStruct((LATER, 2, vocab, tok // 2), BF16),
             ),
             in_specs=[any_spec, vmem_spec, any_spec],
-            out_specs=(vmem_spec, any_spec, any_spec),
+            out_specs=(vmem_spec, any_spec, any_spec, any_spec),
             scratch_shapes=[
                 pltpu.VMEM((2, vocab, dim), BF16),
                 pltpu.VMEM((vocab, dim), F32),
                 pltpu.VMEM((4, 2 * side, side, ROWS, dim), BF16),
                 pltpu.VMEM((2, vocab, tok), F32),
-                pltpu.VMEM((2, vocab, tok // 2), BF16),
+                pltpu.VMEM((2, 2, vocab, tok // 2), BF16),
                 pltpu.VMEM((2, vocab, tok // 2), BF16),
                 pltpu.VMEM((2, side, side * ROWS, dim), F32),
                 pltpu.VMEM((2, side, ROWS, dim), F32),
@@ -393,14 +436,30 @@
                 dma((2,)), dma((2,)),
                 dma((2, side - 1)), dma((2, side - 1)),
                 dma((2, side - 1)), dma((2, side - 1)),
-                dma((2,)), dma,
+                dma((2,)), dma, dma,
             ],
             compiler_params=pltpu.CompilerParams(
                 collective_id=0, has_side_effects=True, vmem_limit_bytes=67043328,
             ),
             name="head",
         )(hid, tgt, w_blk)
-        return loss[0, :1], dh.reshape(tokens // group, dim), dw
+        steps, cols = 8, dim // 8
+        rows = tokens // group // steps
+        stride = chunks // (LATER + 1)
+        dw_spec, dh_spec = pl.BlockSpec((vocab, cols), lambda j: (0, j)), pl.BlockSpec((rows, dim), lambda j: (j, 0))
+        h_specs = [
+            pl.BlockSpec((side, side, 2, 1, ROWS, cols), lambda j, k=k: (0, 0, 0, (k + 1) * stride - 1, 0, j)) for k in range(LATER)
+        ]
+        dw, dh = pl.pallas_call(
+            functools.partial(last_kernel, side),
+            grid=(steps,),
+            out_shape=(jax.ShapeDtypeStruct((vocab, dim), F32), jax.ShapeDtypeStruct((tokens // group, dim), F32)),
+            in_specs=[dw_spec, dh_spec, pl.BlockSpec((LATER, 2, vocab, tok // 2), lambda j: (0, 0, 0, 0)), *h_specs],
+            out_specs=(dw_spec, dh_spec),
+            compiler_params=pltpu.CompilerParams(dimension_semantics=("arbitrary",), vmem_limit_bytes=48 << 20),
+            name="last",
+        )(dw, dh.reshape(tokens // group, dim), dz_left, *[hid] * LATER)
+        return loss[0, :1], dh, dw
 
     return jax.shard_map(
         local_step,

time: 448 us -> 455 us (1.016)
  Pallas kernels: 427 us -> 448 us
  local copies, waits for them, and re-layouts: 17.7 us -> 3.66 us
    pallas_call x0 -> x1, Pallas kernels: none -> 19 us  [local_step(): pl.pallas_call(functools.partial(last_kernel, side), grid=(steps,), out_s...]
    unnamed x2 -> x4, local copies, waits for them, and re-layouts: 16.2 us -> 2.18 us
where the time goes in v1:
time: 455 us; the launch traced here: 454 us
  Pallas kernels  448 us (98%)
    pallas_call x1, Pallas kernels, local_step(): pl.pallas_call(functools.partial(head_kernel, group, side, chunks, tokens...  429 us
    pallas_call x1, Pallas kernels, local_step(): pl.pallas_call(functools.partial(last_kernel, side), grid=(steps,), out_s...  19 us

profile of v1, /device:TPU:96, one launch (start us, length us, event | category | flops | bytes accessed | tf_op | source)
XLA Modules:
  0.0 454.4 jit_solution(12272874234879011846)
XLA Ops:
  0.6 1.0 reshape.22
  1.7 0.1 copy.7
  1.8 0.1 copy.9
  1.9 0.1 copy.8
  2.0 0.1 copy.10
  2.1 0.7 pad_add_fusion.tgt
  2.8 429.2 %head.1 = (f32[1,128]{1,0:T(1,128)}, f32[32,16,2048]{2,1,0:T(8,128)}, f32[1536,2048]{1,0:T(8,128)}, bf16[3,2,1536,256]{3,2,1,0:T(8,128)(2,1)}) custom-call(bf16[4,4,2,32,16,2048]{5,4,3,2,1,0:T(8,128)(2,1)} %bitcast.hid.rest_0_.rest_1_.rest_2_, s32[32,1,512]{2,1,0:T(1,128)} %pad_add_fusion.tgt, bf16[1536,2048]{1,0:T(8,128)(2,1)} %w_hbm.1), custom_call_target="tpu_custom_call" | custom-call | tf_op jit(solution)/shard_map/head/pallas_call | solution.py:402
  432.0 0.0 copy-start
  432.0 2.2 copy-done
  434.2 0.0 copy-start.1
  434.2 19.0 %last.1 = (f32[1536,2048]{1,0:T(8,128)}, f32[512,2048]{1,0:T(8,128)}) custom-call(f32[1536,2048]{1,0:T(8,128)} %get-tuple-element.10.dw_ref, f32[512,2048]{1,0:T(8,128)S(1)} %bitcast.14, bf16[3,2,1536,256]{3,2,1,0:T(8,128)(2,1)} %get-tuple-element.12.dz_ref, bf16[4,4,2,32,16,2048]{5,4,3,2,1,0:T(8,128)(2,1)} %bitcast.hid.rest_0_.rest_1_.rest_2_, ...), custom_call_target="tpu_custom_call" | custom-call | tf_op jit(solution)/shard_map/last/pallas_call | solution.py:453
  453.2 0.0 copy-done.1
  (1 shorter events, 0.0 us)
Async XLA Ops:
  432.0 2.2 copy-start
  434.2 19.0 %copy-start.1 = (f32[1,128]{1,0:T(1,128)S(1)}, f32[1,128]{1,0:T(1,128)}, u32[]{:S(2)}) copy-start(f32[1,128]{1,0:T(1,128)} %get-tuple-element.9) | copy-start | bytes 1540

commit v2 on v1

--- a/solution.py
+++ b/solution.py
@@ -12,7 +12,7 @@
 BF16 = jnp.bfloat16
 LOG2E = 1.4426950408889634
 LN2 = 0.6931471805599453
-LATER = 3
+LATER = 2
 ROWS = 16
 AXIS = "fsdp"
 
@@ -85,7 +85,7 @@
         pl.when(cond)(fn)
 
     barrier = pltpu.get_barrier_semaphore()
-    friends = [partner, *peers_x, *peers_y]
+    friends = [partner] + [peer + o for peer in (*peers_x, *peers_y) for o in (0, 1 - 2 * core)]
     for dev in friends:
         pl.semaphore_signal(barrier, inc=1, device_id={AXIS: dev}, device_id_type=pl.DeviceIdType.MESH)
 
@@ -148,17 +148,17 @@
 
     def st1_copy(i):
         s = lax.rem(i, 2)
-        return [
-            rcopy(mid.at[s], st1.at[s, x], st1_send.at[s, k], st1_recv.at[s, k], peer)
-            for k, peer in enumerate(peers_x)
-        ]
+        to = [(peer - o, k) for k, peer in enumerate(peers_x) for o in (0, 1)] + [(partner, side - 1)]
+        return [rcopy(mid.at[s], st1.at[s, x], st1_send.at[s, n], st1_recv.at[s, k], dev) for n, (dev, k) in enumerate(to)]
 
     def st2_copy(i):
         s = lax.rem(i, 2)
-        return [
-            rcopy(row.at[s], st2.at[s, y], st2_send.at[s, k], st2_recv.at[s, k], peer)
-            for k, peer in enumerate(peers_y)
-        ]
+        to = [(peer + o, k) for k, peer in enumerate(peers_y) for o in (0, 1)] + [(partner, side - 1)]
+        return [rcopy(row.at[s], st2.at[s, y], st2_send.at[s, n], st2_recv.at[s, k], dev) for n, (dev, k) in enumerate(to)]
+
+    def st_wait(copies, partner_core):
+        wait_recv(copies[0:-1:2])
+        guarded(core == partner_core, lambda: wait_recv(copies[-1:]))
 
     def two(fn):
         lax.fori_loop(0, 2, lambda j, carry: (fn(j), carry)[1], 0)
@@ -233,32 +233,41 @@
 
     def st_own(i):
         s = lax.rem(i, 2)
-        guarded(i >= 2, lambda: wait_send(st0_copy(i)))
+
+        @pl.when(core == 0)
+        def _():
+            guarded(i >= 2, lambda: wait_send(st0_copy(i)))
+
         own[s, 0:1, :] = join([stat[0, 0:1, :], stat[1, 0:1, :]])
         own[s, 1:2, :] = stat[0, 1:2, :] + stat[1, 1:2, :]
-        start(st0_copy(i))
+        guarded(core == 0, lambda: start(st0_copy(i)))
 
     def st_pair(i):
         s = lax.rem(i, 2)
-        wait_recv(st0_copy(i))
-        guarded(i >= 2, lambda: wait_send(st1_copy(i)))
-        mid[s, 0:1, :] = join([own[s, 0:1, :], st0[s, 0:1, :]])
-        mid[s, 1:2, :] = own[s, 1:2, :] + st0[s, 1:2, :]
-        st1[s, x] = mid[s]
-        start(st1_copy(i))
+
+        @pl.when(core == 1)
+        def _():
+            wait_recv(st0_copy(i))
+            guarded(i >= 2, lambda: wait_send(st1_copy(i)))
+            mid[s, 0:1, :] = join([st0[s, 0:1, :], own[s, 0:1, :]])
+            mid[s, 1:2, :] = st0[s, 1:2, :] + own[s, 1:2, :]
+            start(st1_copy(i))
 
     def st_row(i):
         s = lax.rem(i, 2)
-        wait_recv(st1_copy(i))
-        guarded(i >= 2, lambda: wait_send(st2_copy(i)))
-        row[s, 0:1, :] = join([st1[s, k, 0:1, :] for k in range(side)])
-        row[s, 1:2, :] = functools.reduce(jnp.add, [st1[s, k, 1:2, :] for k in range(side)])
-        st2[s, y] = row[s]
-        start(st2_copy(i))
+        st_wait(st1_copy(i), 0)
+
+        @pl.when(core == 0)
+        def _():
+            guarded(i >= 2, lambda: wait_send(st2_copy(i)))
+            row[s, 0:1, :] = join([st1[s, k, 0:1, :] for k in range(side)])
+            row[s, 1:2, :] = functools.reduce(jnp.add, [st1[s, k, 1:2, :] for k in range(side)])
+            st2[s, y] = row[s]
+            start(st2_copy(i))
 
     def st_all(i):
         s = lax.rem(i, 2)
-        wait_recv(st2_copy(i))
+        st_wait(st2_copy(i), 1)
         full = join([st2[s, k, 0:1, :] for k in range(side)])
         hit = functools.reduce(jnp.add, [st2[s, k, 1:2, :] for k in range(side)])
         lse[0:1, :] = full + math.log2(tokens)
@@ -337,6 +346,7 @@
             wait_recv(dz_copy(c))
             grad_h(c)
 
+        guarded(live(i - 1), lambda: st_all(i - 1))
         guarded(has_a, lambda: st_pair(i))
 
         @pl.when(has_c)
@@ -348,8 +358,6 @@
         def _():
             pltpu.make_async_copy(dz.at[lax.rem(c + 2, 2)], dz_hbm.at[c // stride], dxsem).wait()
 
-        guarded(live(i - 1), lambda: st_all(i - 1))
-
         @pl.when(c == chunks)
         def _():
             two(lambda j: grad_w(c - 1, j))
@@ -360,7 +368,8 @@
     lax.fori_loop(0, chunks + 5, step, 0)
 
     for i in range(max(chunks - 2, 0), chunks):
-        wait_send(st0_copy(i) + st1_copy(i) + st2_copy(i))
+        guarded(core == 0, lambda: wait_send(st0_copy(i) + st2_copy(i)))
+        guarded(core == 1, lambda: wait_send(st1_copy(i)))
         pltpu.make_async_copy(ob.at[i % 2], dh_hbm.at[i], osem.at[i % 2]).wait()
     w_remote.wait_send()
     pltpu.make_async_copy(dwacc, dw_hbm, dwsem).wait()
@@ -434,8 +443,8 @@
                 dma((6, 2, 2)), dma((6, 2, 2)),
                 dma, dma((2,)), dma, dma,
                 dma((2,)), dma((2,)),
-                dma((2, side - 1)), dma((2, side - 1)),
-                dma((2, side - 1)), dma((2, side - 1)),
+                dma((2, 2 * side - 1)), dma((2, side)),
+                dma((2, 2 * side - 1)), dma((2, side)),
                 dma((2,)), dma, dma,
             ],
             compiler_params=pltpu.CompilerParams(
@@ -443,20 +452,20 @@
             ),
             name="head",
         )(hid, tgt, w_blk)
-        steps, cols = 8, dim // 8
-        rows = tokens // group // steps
+        steps = 8
         stride = chunks // (LATER + 1)
-        dw_spec, dh_spec = pl.BlockSpec((vocab, cols), lambda j: (0, j)), pl.BlockSpec((rows, dim), lambda j: (j, 0))
+        dw_spec, dh_spec = [pl.BlockSpec((n // steps, dim), lambda j: (j, 0)) for n in (vocab, tokens // group)]
+        dz_spec = pl.BlockSpec((LATER, 2, vocab // steps, tok // 2), lambda j: (0, 0, j, 0))
         h_specs = [
-            pl.BlockSpec((side, side, 2, 1, ROWS, cols), lambda j, k=k: (0, 0, 0, (k + 1) * stride - 1, 0, j)) for k in range(LATER)
+            pl.BlockSpec((side, side, 2, 1, ROWS, dim), lambda j, k=k: (0, 0, 0, (k + 1) * stride - 1, 0, 0)) for k in range(LATER)
         ]
         dw, dh = pl.pallas_call(
             functools.partial(last_kernel, side),
             grid=(steps,),
             out_shape=(jax.ShapeDtypeStruct((vocab, dim), F32), jax.ShapeDtypeStruct((tokens // group, dim), F32)),
-            in_specs=[dw_spec, dh_spec, pl.BlockSpec((LATER, 2, vocab, tok // 2), lambda j: (0, 0, 0, 0)), *h_specs],
+            in_specs=[dw_spec, dh_spec, dz_spec, *h_specs],
             out_specs=(dw_spec, dh_spec),
-            compiler_params=pltpu.CompilerParams(dimension_semantics=("arbitrary",), vmem_limit_bytes=48 << 20),
+            compiler_params=pltpu.CompilerParams(dimension_semantics=("arbitrary",), vmem_limit_bytes=67043328),
             name="last",
         )(dw, dh.reshape(tokens // group, dim), dz_left, *[hid] * LATER)
         return loss[0, :1], dh, dw

time: 455 us -> 454 us (level)
  no operation moved by 1% of the time
where the time goes in v2:
time: 454 us; the launch traced here: 453 us
  Pallas kernels  449 us (99%)
    pallas_call x1, Pallas kernels, local_step(): pl.pallas_call(functools.partial(head_kernel, group, side, chunks, tokens...  430 us
    pallas_call x1, Pallas kernels, local_step(): pl.pallas_call(functools.partial(last_kernel, side), grid=(steps,), out_s...  18.7 us

profile of v2, /device:TPU:96, one launch (start us, length us, event | category | flops | bytes accessed | tf_op | source)
XLA Modules:
  0.0 453.2 jit_solution(8592792437156421384)
XLA Ops:
  0.6 1.0 reshape.22
  1.7 0.1 copy.7
  1.8 0.1 copy.9
  1.9 0.1 copy.8
  2.0 0.1 copy.10
  2.1 0.7 pad_add_fusion.tgt
  2.8 429.9 %head.1 = (f32[1,128]{1,0:T(1,128)}, f32[32,16,2048]{2,1,0:T(8,128)}, f32[1536,2048]{1,0:T(8,128)}, bf16[2,2,1536,256]{3,2,1,0:T(8,128)(2,1)}) custom-call(bf16[4,4,2,32,16,2048]{5,4,3,2,1,0:T(8,128)(2,1)} %bitcast.hid.rest_0_.rest_1_, s32[32,1,512]{2,1,0:T(1,128)} %pad_add_fusion.tgt, bf16[1536,2048]{1,0:T(8,128)(2,1)} %w_hbm.1), custom_call_target="tpu_custom_call" | custom-call | tf_op jit(solution)/shard_map/head/pallas_call | solution.py:411
  432.7 18.7 %last.1 = (f32[1536,2048]{1,0:T(8,128)}, f32[512,2048]{1,0:T(8,128)}) custom-call(f32[1536,2048]{1,0:T(8,128)} %get-tuple-element.10.dw_ref, f32[512,2048]{1,0:T(8,128)} %bitcast.14, bf16[2,2,1536,256]{3,2,1,0:T(8,128)(2,1)} %get-tuple-element.12.dz_ref, bf16[4,4,2,32,16,2048]{5,4,3,2,1,0:T(8,128)(2,1)} %bitcast.hid.rest_0_.rest_1_, ...), custom_call_target="tpu_custom_call" | custom-call | tf_op jit(solution)/shard_map/last/pallas_call | solution.py:462
  (1 shorter events, 0.0 us)

commit v3 on v2

--- a/solution.py
+++ b/solution.py
@@ -12,7 +12,6 @@
 BF16 = jnp.bfloat16
 LOG2E = 1.4426950408889634
 LN2 = 0.6931471805599453
-LATER = 2
 ROWS = 16
 AXIS = "fsdp"
 
@@ -40,16 +39,15 @@
 def head_kernel(
     group, side, chunks, tokens,
     hid, tgt, w_hbm,
-    loss_ref, dh_hbm, dw_hbm, dz_hbm,
+    loss_ref, dh_hbm, dw_hbm,
     wb, dwacc, hb, yb, dz, dzr, sb, tb, far1, pure1, merged1, far2, pure2, merged2, ob,
     stat, own, st0, mid, st1, row, st2, lse, lossacc,
     wsem, hsem, rs_send, rs_recv, dz_send, dz_recv, w_send, w_recv,
-    st0_send, st0_recv, st1_send, st1_recv, st2_send, st2_recv, osem, dwsem, dxsem,
+    st0_send, st0_recv, st1_send, st1_recv, st2_send, st2_recv, osem, dwsem,
 ):
     vocab, dim = w_hbm.shape
     half = dim // 2
     mt = vocab // 2
-    stride = chunks // (LATER + 1)
     tok = hb.shape[1] * hb.shape[2] * ROWS
     tokc = tok // 2
 
@@ -81,8 +79,22 @@
             device_id={AXIS: dev}, device_id_type=pl.DeviceIdType.MESH,
         )
 
+    steady = [False]
+
     def guarded(cond, fn):
-        pl.when(cond)(fn)
+        if steady[0]:
+            fn()
+        else:
+            pl.when(cond)(lambda: (fn(), None)[1])
+
+    def both_ways(cond, fn):
+        @pl.when(cond)
+        def _():
+            steady[0] = True
+            fn()
+            steady[0] = False
+
+        pl.when(jnp.logical_not(cond))(fn)
 
     barrier = pltpu.get_barrier_semaphore()
     friends = [partner] + [peer + o for peer in (*peers_x, *peers_y) for o in (0, 1 - 2 * core)]
@@ -116,13 +128,15 @@
     w_remote.start()
 
     def rs(kind, c):
-        s = lax.rem(c, 2)
+        s = t = lax.rem(c, 2)
+        if kind >= FAR2:
+            t = lax.rem(c, 3)
         lo, hi = pl.ds(0, half), pl.ds(half, half)
         buf, to, (up, down, far) = (sb, to_p, near_p) if kind < 3 else (tb, to_q, near_q)
         dst = (far1, pure1, merged1, far2, pure2, merged2)[kind]
         src = {0: ((far, lo), (far, hi)), 1: ((up, hi), (down, lo)), 2: ((up, lo), (down, hi))}[kind % 3]
         return [
-            rcopy(buf.at[s, src[d][0], :, src[d][1]], dst.at[s, d], rs_send.at[kind, s, d], rs_recv.at[kind, s, d], to[d])
+            rcopy(buf.at[s, src[d][0], :, src[d][1]], dst.at[t, d], rs_send.at[kind, t, d], rs_recv.at[kind, t, d], to[d])
             for d in range(2)
         ]
 
@@ -158,7 +172,7 @@
 
     def st_wait(copies, partner_core):
         wait_recv(copies[0:-1:2])
-        guarded(core == partner_core, lambda: wait_recv(copies[-1:]))
+        pl.when(core == partner_core)(lambda: wait_recv(copies[-1:]))
 
     def two(fn):
         lax.fori_loop(0, 2, lambda j, carry: (fn(j), carry)[1], 0)
@@ -201,8 +215,9 @@
         wait_recv(rs(PURE2, c) + rs(MERGED2, c))
         wait_send(rs(FAR2, c) + rs(PURE2, c) + rs(MERGED2, c))
         guarded(c >= 2, lambda: pltpu.make_async_copy(ob.at[s], dh_hbm.at[c - 2], osem.at[s]).wait())
-        ob[s, :, :half] = tb[s, q, :, :half] + merged2[s, 0] + pure2[s, 1]
-        ob[s, :, half:] = tb[s, q, :, half:] + pure2[s, 0] + merged2[s, 1]
+        t = lax.rem(c, 3)
+        ob[s, :, :half] = tb[s, q, :, :half] + merged2[t, 0] + pure2[t, 1]
+        ob[s, :, half:] = tb[s, q, :, half:] + pure2[t, 0] + merged2[t, 1]
         pltpu.make_async_copy(ob.at[s], dh_hbm.at[c], osem.at[s]).start()
 
     def turn(c):
@@ -227,8 +242,9 @@
         s = lax.rem(c, 2)
         up, down, _ = near_q
         wait_recv(rs(FAR2, c))
-        tb[s, up, :, :half] += far2[s, 0]
-        tb[s, down, :, half:] += far2[s, 1]
+        t = lax.rem(c, 3)
+        tb[s, up, :, :half] += far2[t, 0]
+        tb[s, down, :, half:] += far2[t, 1]
         start(rs(MERGED2, c))
 
     def st_own(i):
@@ -240,7 +256,7 @@
 
         own[s, 0:1, :] = join([stat[0, 0:1, :], stat[1, 0:1, :]])
         own[s, 1:2, :] = stat[0, 1:2, :] + stat[1, 1:2, :]
-        guarded(core == 0, lambda: start(st0_copy(i)))
+        pl.when(core == 0)(lambda: start(st0_copy(i)))
 
     def st_pair(i):
         s = lax.rem(i, 2)
@@ -302,16 +318,30 @@
         def live(k):
             return jnp.logical_and(k >= 0, k < chunks)
 
-        @pl.when(has_c)
-        def _():
-            start(dz_copy(c))
-
-        guarded(live(c - 3), lambda: finish(c - 3))
-        guarded(live(c - 2), lambda: turn(c - 2))
-        guarded(live(c - 1), lambda: start(rs(PURE1, c - 1)))
-        later = jnp.logical_and(lax.rem(c, stride) == stride - 1, c // stride < LATER)
-        now = jnp.logical_and(jnp.logical_and(c >= 0, c < chunks - 2), jnp.logical_not(later))
-        save = jnp.logical_and(jnp.logical_and(c >= 0, c < chunks - 2), later)
+        def live(k):
+            return jnp.logical_and(k >= 0, k < chunks)
+
+        calm = jnp.logical_and(i >= 7, i < chunks)
+
+        def point_a():
+            guarded(has_c, lambda: start(dz_copy(c)))
+            guarded(live(c - 2), lambda: turn(c - 2))
+            guarded(live(c - 1), lambda: start(rs(PURE1, c - 1)))
+
+        def point_m():
+            guarded(live(c - 1), lambda: merge1(c - 1))
+            guarded(has_a, lambda: st_own(i))
+            guarded(live(c - 3), lambda: finish(c - 3))
+
+        def point_b():
+            guarded(live(i - 1), lambda: st_all(i - 1))
+            guarded(has_a, lambda: st_pair(i))
+            guarded(has_c, lambda: (start(rs(FAR1, c)), wait_send(dz_copy(c))))
+            guarded(live(c - 2), lambda: merge2(c - 2))
+
+        both_ways(calm, point_a)
+
+        now = jnp.logical_and(c >= 0, c < chunks - 2)
 
         @pl.when(now)
         def _():
@@ -320,43 +350,24 @@
                 grad_w(c, j)
 
             lax.fori_loop(0, one, lambda j, u: (half_dw(j), u)[1], 0)
-            guarded(live(i - 1), lambda: st_row(i - 1))
+            both_ways(calm, lambda: guarded(live(i - 1), lambda: st_row(i - 1)))
             lax.fori_loop(one, 2, lambda j, u: (half_dw(j), u)[1], 0)
 
-        @pl.when(jnp.logical_not(now))
-        def _():
-            @pl.when(save)
-            def _():
-                pltpu.make_async_copy(dz.at[lax.rem(c + 2, 2)], dz_hbm.at[c // stride], dxsem).start()
-                two(lambda j: statistics(i, j, slot))
-
-            guarded(live(i - 1), lambda: st_row(i - 1))
+        pl.when(jnp.logical_and(jnp.logical_not(now), live(i - 1)))(lambda: st_row(i - 1))
 
         @pl.when(c == chunks)
         def _():
             two(lambda j: grad_w(c - 2, j))
 
-        guarded(live(c - 1), lambda: merge1(c - 1))
-        guarded(live(c - 2), lambda: merge2(c - 2))
-        guarded(has_a, lambda: st_own(i))
+        both_ways(calm, point_m)
 
         @pl.when(has_c)
         def _():
-            guarded(c == 0, w_remote.wait_recv)
+            pl.when(c == 0)(w_remote.wait_recv)
             wait_recv(dz_copy(c))
             grad_h(c)
 
-        guarded(live(i - 1), lambda: st_all(i - 1))
-        guarded(has_a, lambda: st_pair(i))
-
-        @pl.when(has_c)
-        def _():
-            start(rs(FAR1, c))
-            wait_send(dz_copy(c))
-
-        @pl.when(save)
-        def _():
-            pltpu.make_async_copy(dz.at[lax.rem(c + 2, 2)], dz_hbm.at[c // stride], dxsem).wait()
+        both_ways(calm, point_b)
 
         @pl.when(c == chunks)
         def _():
@@ -376,16 +387,18 @@
     loss_ref[...] = jnp.broadcast_to(jnp.sum(lossacc[...], axis=1, keepdims=True) * (LN2 / tokens), loss_ref.shape)
 
 
-def last_kernel(side, dw_ref, dh_ref, dz_ref, *rest):
-    hid, (dw_out, dh_out) = rest[:LATER], rest[LATER:]
-    total = dw_ref[...]
-    for k in range(LATER):
-        h = hid[k]
-        by_x = [h[yy, xx, 0, 0] for xx in range(side) for yy in range(side)]
-        by_y = [h[yy, xx, 1, 0] for yy in range(side) for xx in range(side)]
-        total += dot_nn(dz_ref[k, 0], jnp.concatenate(by_x, axis=0)) + dot_nn(dz_ref[k, 1], jnp.concatenate(by_y, axis=0))
-    dw_out[...] = total
-    dh_out[...] = dh_ref[...]
+def copy_kernel(dw_hbm, dh_hbm, dw_out, dh_out, buf, isem, osem):
+    rows = buf.shape[1]
+    pieces = [(src.at[pl.ds(r, rows)], dst.at[pl.ds(r, rows)]) for src, dst in ((dw_hbm, dw_out), (dh_hbm, dh_out)) for r in range(0, src.shape[0], rows)]
+    get = [pltpu.make_async_copy(src, buf.at[k], isem.at[k]) for k, (src, _) in enumerate(pieces)]
+    put = [pltpu.make_async_copy(buf.at[k], dst, osem.at[k]) for k, (_, dst) in enumerate(pieces)]
+    for copy in get:
+        copy.start()
+    for copy, back in zip(get, put):
+        copy.wait()
+        back.start()
+    for back in put:
+        back.wait()
 
 
 def solution(mesh):
@@ -407,17 +420,16 @@
         dma = pltpu.SemaphoreType.DMA
         any_spec = pl.BlockSpec(memory_space=pl.ANY)
         vmem_spec = pl.BlockSpec(memory_space=pltpu.VMEM)
-        big, small = (2, 2, side * ROWS, half), (2, 2, ROWS, half)
-        loss, dh, dw, dz_left = pl.pallas_call(
+        big, small = (2, 2, side * ROWS, half), (3, 2, ROWS, half)
+        loss, dh, dw = pl.pallas_call(
             functools.partial(head_kernel, group, side, chunks, tokens),
             out_shape=(
                 jax.ShapeDtypeStruct((1, 128), F32),
                 jax.ShapeDtypeStruct((chunks, ROWS, dim), F32),
                 jax.ShapeDtypeStruct((vocab, dim), F32),
-                jax.ShapeDtypeStruct((LATER, 2, vocab, tok // 2), BF16),
             ),
             in_specs=[any_spec, vmem_spec, any_spec],
-            out_specs=(vmem_spec, any_spec, any_spec, any_spec),
+            out_specs=(vmem_spec, any_spec, any_spec),
             scratch_shapes=[
                 pltpu.VMEM((2, vocab, dim), BF16),
                 pltpu.VMEM((vocab, dim), F32),
@@ -440,34 +452,29 @@
                 pltpu.VMEM((1, tok), F32),
                 pltpu.VMEM((1, tok), F32),
                 dma, dma((4,)),
-                dma((6, 2, 2)), dma((6, 2, 2)),
+                dma((6, 3, 2)), dma((6, 3, 2)),
                 dma, dma((2,)), dma, dma,
                 dma((2,)), dma((2,)),
                 dma((2, 2 * side - 1)), dma((2, side)),
                 dma((2, 2 * side - 1)), dma((2, side)),
-                dma((2,)), dma, dma,
+                dma((2,)), dma,
             ],
             compiler_params=pltpu.CompilerParams(
                 collective_id=0, has_side_effects=True, vmem_limit_bytes=67043328,
             ),
             name="head",
         )(hid, tgt, w_blk)
-        steps = 8
-        stride = chunks // (LATER + 1)
-        dw_spec, dh_spec = [pl.BlockSpec((n // steps, dim), lambda j: (j, 0)) for n in (vocab, tokens // group)]
-        dz_spec = pl.BlockSpec((LATER, 2, vocab // steps, tok // 2), lambda j: (0, 0, j, 0))
-        h_specs = [
-            pl.BlockSpec((side, side, 2, 1, ROWS, dim), lambda j, k=k: (0, 0, 0, (k + 1) * stride - 1, 0, 0)) for k in range(LATER)
-        ]
+        rows = tokens // group // 4
+        pieces = (vocab + tokens // group) // rows
         dw, dh = pl.pallas_call(
-            functools.partial(last_kernel, side),
-            grid=(steps,),
+            copy_kernel,
             out_shape=(jax.ShapeDtypeStruct((vocab, dim), F32), jax.ShapeDtypeStruct((tokens // group, dim), F32)),
-            in_specs=[dw_spec, dh_spec, dz_spec, *h_specs],
-            out_specs=(dw_spec, dh_spec),
-            compiler_params=pltpu.CompilerParams(dimension_semantics=("arbitrary",), vmem_limit_bytes=67043328),
-            name="last",
-        )(dw, dh.reshape(tokens // group, dim), dz_left, *[hid] * LATER)
+            in_specs=[any_spec] * 2,
+            out_specs=(any_spec, any_spec),
+            scratch_shapes=[pltpu.VMEM((pieces, rows, dim), F32), dma((pieces,)), dma((pieces,))],
+            compiler_params=pltpu.CompilerParams(vmem_limit_bytes=67043328),
+            name="results",
+        )(dw, dh.reshape(tokens // group, dim))
         return loss[0, :1], dh, dw
 
     return jax.shard_map(

time: 454 us -> 440 us (0.969)
  Pallas kernels: 449 us -> 435 us
    pallas_call x1, Pallas kernels: 18.7 us -> 12 us  [local_step(): pl.pallas_call(copy_kernel, out_shape=(jax.ShapeDtypeStruct((vocab, dim),...]
    pallas_call x1, Pallas kernels: 430 us -> 423 us  [local_step(): pl.pallas_call(functools.partial(head_kernel, group, side, chunks, tokens...]
where the time goes in v3:
time: 440 us
  Pallas kernels  435 us (99%)
    pallas_call x1, Pallas kernels, local_step(): pl.pallas_call(functools.partial(head_kernel, group, side, chunks, tokens...  423 us
    pallas_call x1, Pallas kernels, local_step(): pl.pallas_call(copy_kernel, out_shape=(jax.ShapeDtypeStruct((vocab, dim),...  12 us

profile of v3, /device:TPU:96, one launch (start us, length us, event | category | flops | bytes accessed | tf_op | source)
XLA Modules:
  0.0 439.7 jit_solution(14705180610540276643)
XLA Ops:
  0.6 1.0 reshape.22
  1.7 0.1 copy.7
  1.8 0.1 copy.9
  1.9 0.1 copy.8
  2.0 0.1 copy.10
  2.1 0.7 pad_add_fusion.tgt
  2.8 423.2 %head.1 = (f32[1,128]{1,0:T(1,128)}, f32[32,16,2048]{2,1,0:T(8,128)}, f32[1536,2048]{1,0:T(8,128)}) custom-call(bf16[4,4,2,32,16,2048]{5,4,3,2,1,0:T(8,128)(2,1)} %bitcast.hid, s32[32,1,512]{2,1,0:T(1,128)} %pad_add_fusion.tgt, bf16[1536,2048]{1,0:T(8,128)(2,1)} %w_hbm.1), custom_call_target="tpu_custom_call" | custom-call | tf_op jit(solution)/shard_map/head/pallas_call | solution.py:424
  426.0 12.0 %results.1 = (f32[1536,2048]{1,0:T(8,128)}, f32[512,2048]{1,0:T(8,128)}) custom-call(f32[1536,2048]{1,0:T(8,128)} %get-tuple-element.9.dw_hbm, f32[512,2048]{1,0:T(8,128)} %bitcast.14), custom_call_target="tpu_custom_call" | custom-call | tf_op jit(solution)/shard_map/results/pallas_call | solution.py:469
  (1 shorter events, 0.0 us)

commit v4 on v3

--- a/solution.py
+++ b/solution.py
@@ -12,6 +12,7 @@
 BF16 = jnp.bfloat16
 LOG2E = 1.4426950408889634
 LN2 = 0.6931471805599453
+LATE = 2
 ROWS = 16
 AXIS = "fsdp"
 
@@ -34,6 +35,11 @@
     top = functools.reduce(jnp.maximum, parts)
     total = functools.reduce(jnp.add, [jnp.exp2(v - top) for v in parts])
     return top + jnp.log(total) * LOG2E
+
+
+class Chunk:
+    def __init__(self, n, two, three):
+        self.n, self.two, self.three = n, two, three
 
 
 def head_kernel(
@@ -101,36 +107,27 @@
     for dev in friends:
         pl.semaphore_signal(barrier, inc=1, device_id={AXIS: dev}, device_id_type=pl.DeviceIdType.MESH)
 
-    def h_copies(c):
-        s = lax.rem(c, 4)
-        out = []
+    def h_start(n, s):
         for k in range(side):
-            out.append(pltpu.make_async_copy(hid.at[:, k, 0, c], hb.at[s, k], hsem.at[s]))
-            out.append(pltpu.make_async_copy(hid.at[k, :, 1, c], hb.at[s, side + k], hsem.at[s]))
-        return out
-
-    def h_start(c):
-        for d in h_copies(c):
-            d.start()
-
-    def h_wait(c):
-        s = lax.rem(c, 4)
+            pltpu.make_async_copy(hid.at[:, k, 0, n], hb.at[s, k], hsem.at[s]).start()
+            pltpu.make_async_copy(hid.at[k, :, 1, n], hb.at[s, side + k], hsem.at[s]).start()
+
+    def h_wait(s):
         pltpu.make_async_copy(hb.at[s], hb.at[s], hsem.at[s]).wait()
 
-    w_local = pltpu.make_async_copy(w_hbm, wb.at[core], wsem)
-    w_local.start()
-    h_start(0)
+    w_local = [
+        pltpu.make_async_copy(w_hbm.at[pl.ds(k * mt, mt)], wb.at[core, pl.ds(k * mt, mt)], wsem.at[k]) for k in range(2)
+    ]
+    w_local[0].start()
+    h_start(0, 0)
+    w_local[1].start()
     dwacc[...] = jnp.zeros_like(dwacc)
     lossacc[...] = jnp.zeros_like(lossacc)
-    pl.semaphore_wait(barrier, len(friends))
-    w_local.wait()
+    w_local[0].wait()
     w_remote = rcopy(wb.at[core], wb.at[core], w_send, w_recv, partner)
-    w_remote.start()
 
     def rs(kind, c):
-        s = t = lax.rem(c, 2)
-        if kind >= FAR2:
-            t = lax.rem(c, 3)
+        s, t = c.two, c.three if kind >= FAR2 else c.two
         lo, hi = pl.ds(0, half), pl.ds(half, half)
         buf, to, (up, down, far) = (sb, to_p, near_p) if kind < 3 else (tb, to_q, near_q)
         dst = (far1, pure1, merged1, far2, pure2, merged2)[kind]
@@ -153,20 +150,19 @@
             d.wait_send()
 
     def dz_copy(c):
-        s = lax.rem(c, 2)
-        return [rcopy(dz.at[s, other], dzr.at[s], dz_send, dz_recv.at[s], partner)]
-
-    def st0_copy(i):
-        s = lax.rem(i, 2)
+        return [rcopy(dz.at[c.three, other], dzr.at[c.two], dz_send, dz_recv.at[c.two], partner)]
+
+    def st0_copy(c):
+        s = c.two
         return [rcopy(own.at[s], st0.at[s], st0_send.at[s], st0_recv.at[s], partner)]
 
-    def st1_copy(i):
-        s = lax.rem(i, 2)
+    def st1_copy(c):
+        s = c.two
         to = [(peer - o, k) for k, peer in enumerate(peers_x) for o in (0, 1)] + [(partner, side - 1)]
         return [rcopy(mid.at[s], st1.at[s, x], st1_send.at[s, n], st1_recv.at[s, k], dev) for n, (dev, k) in enumerate(to)]
 
-    def st2_copy(i):
-        s = lax.rem(i, 2)
+    def st2_copy(c):
+        s = c.two
         to = [(peer + o, k) for k, peer in enumerate(peers_y) for o in (0, 1)] + [(partner, side - 1)]
         return [rcopy(row.at[s], st2.at[s, y], st2_send.at[s, n], st2_recv.at[s, k], dev) for n, (dev, k) in enumerate(to)]
 
@@ -177,51 +173,48 @@
     def two(fn):
         lax.fori_loop(0, 2, lambda j, carry: (fn(j), carry)[1], 0)
 
-    def logits(i, j, slot):
+    def logits(c, j):
         r = pl.ds(pl.multiple_of(j * mt, mt), mt)
-        h = hb[lax.rem(i, 4)].reshape(tok, dim)
-        yb[slot, r, :] = dot_nt(wb[core, r, :], h) * LOG2E
-
-    def grad_logits(c, j, slot):
+        h = hb[c.two].reshape(tok, dim)
+        yb[c.two, r, :] = dot_nt(wb[core, r, :], h) * LOG2E
+
+    def grad_logits(c, j):
         r = pl.ds(pl.multiple_of(j * mt, mt), mt)
-        prob = jnp.exp2(yb[slot, r, :] - lse[0:1, :])
-        hit = lax.broadcasted_iota(jnp.int32, prob.shape, 0) == tgt[c] - (me * vocab + j * mt)
+        prob = jnp.exp2(yb[c.two, r, :] - lse[0:1, :])
+        hit = lax.broadcasted_iota(jnp.int32, prob.shape, 0) == tgt[c.n] - (me * vocab + j * mt)
         g = (prob + jnp.where(hit, -1.0 / tokens, 0.0)).astype(BF16)
-        dz[slot, 0, r, :] = g[:, :tokc]
-        dz[slot, 1, r, :] = g[:, tokc:]
-
-    def statistics(i, j, slot):
-        v = yb[slot, pl.ds(pl.multiple_of(j * mt, mt), mt), :]
+        dz[c.three, 0, r, :] = g[:, :tokc]
+        dz[c.three, 1, r, :] = g[:, tokc:]
+
+    def statistics(c, j):
+        v = yb[c.two, pl.ds(pl.multiple_of(j * mt, mt), mt), :]
         top = jnp.max(v, axis=0, keepdims=True)
         total = jnp.sum(jnp.exp2(v - top), axis=0, keepdims=True)
-        hit = lax.broadcasted_iota(jnp.int32, v.shape, 0) == tgt[lax.rem(i, chunks)] - (me * vocab + j * mt)
+        hit = lax.broadcasted_iota(jnp.int32, v.shape, 0) == tgt[lax.rem(c.n, chunks)] - (me * vocab + j * mt)
         stat[j, 0:1, :] = top + jnp.log(total) * LOG2E
         stat[j, 1:2, :] = jnp.sum(jnp.where(hit, v, 0.0), axis=0, keepdims=True)
 
     def grad_w(c, k):
         n = dim // 2
         cols = pl.ds(pl.multiple_of(k * n, n), n)
-        h = hb[lax.rem(c, 4), :, :, :, cols].reshape(tok, n)
-        s = lax.rem(c, 2)
-        dwacc[:, cols] += dot_nn(dz[s, 0], h[:tokc]) + dot_nn(dz[s, 1], h[tokc:])
+        h = hb[2 + c.two, :, :, :, cols].reshape(tok, n)
+        dwacc[:, cols] += dot_nn(dz[c.three, 0], h[:tokc]) + dot_nn(dz[c.three, 1], h[tokc:])
 
     def grad_h(c):
-        s = lax.rem(c, 2)
-        v = dot_tn(dz[s, core], wb[core]) + dot_tn(dzr[s], wb[other])
-        sb[s] = v.reshape(side, side * ROWS, dim)
+        v = dot_tn(dz[c.three, core], wb[core]) + dot_tn(dzr[c.two], wb[other])
+        sb[c.two] = v.reshape(side, side * ROWS, dim)
 
     def finish(c):
-        s = lax.rem(c, 2)
+        s, t = c.two, c.three
         wait_recv(rs(PURE2, c) + rs(MERGED2, c))
         wait_send(rs(FAR2, c) + rs(PURE2, c) + rs(MERGED2, c))
-        guarded(c >= 2, lambda: pltpu.make_async_copy(ob.at[s], dh_hbm.at[c - 2], osem.at[s]).wait())
-        t = lax.rem(c, 3)
+        guarded(c.n >= 2, lambda: pltpu.make_async_copy(ob.at[s], dh_hbm.at[c.n - 2], osem.at[s]).wait())
         ob[s, :, :half] = tb[s, q, :, :half] + merged2[t, 0] + pure2[t, 1]
         ob[s, :, half:] = tb[s, q, :, half:] + pure2[t, 0] + merged2[t, 1]
-        pltpu.make_async_copy(ob.at[s], dh_hbm.at[c], osem.at[s]).start()
+        pltpu.make_async_copy(ob.at[s], dh_hbm.at[c.n], osem.at[s]).start()
 
     def turn(c):
-        s = lax.rem(c, 2)
+        s = c.two
         wait_recv(rs(PURE1, c) + rs(MERGED1, c))
         lo = sb[s, p, :, :half] + merged1[s, 0] + pure1[s, 1]
         hi = sb[s, p, :, half:] + pure1[s, 0] + merged1[s, 1]
@@ -231,7 +224,7 @@
         wait_send(rs(FAR1, c) + rs(PURE1, c) + rs(MERGED1, c))
 
     def merge1(c):
-        s = lax.rem(c, 2)
+        s = c.two
         up, down, _ = near_p
         wait_recv(rs(FAR1, c))
         sb[s, up, :, :half] += far1[s, 0]
@@ -239,139 +232,156 @@
         start(rs(MERGED1, c))
 
     def merge2(c):
-        s = lax.rem(c, 2)
+        s, t = c.two, c.three
         up, down, _ = near_q
         wait_recv(rs(FAR2, c))
-        t = lax.rem(c, 3)
         tb[s, up, :, :half] += far2[t, 0]
         tb[s, down, :, half:] += far2[t, 1]
         start(rs(MERGED2, c))
 
-    def st_own(i):
-        s = lax.rem(i, 2)
+    def st_own(c):
+        s = c.two
 
         @pl.when(core == 0)
         def _():
-            guarded(i >= 2, lambda: wait_send(st0_copy(i)))
+            guarded(c.n >= 2, lambda: wait_send(st0_copy(c)))
 
         own[s, 0:1, :] = join([stat[0, 0:1, :], stat[1, 0:1, :]])
         own[s, 1:2, :] = stat[0, 1:2, :] + stat[1, 1:2, :]
-        pl.when(core == 0)(lambda: start(st0_copy(i)))
-
-    def st_pair(i):
-        s = lax.rem(i, 2)
+        pl.when(core == 0)(lambda: start(st0_copy(c)))
+
+    def st_pair(c):
+        s = c.two
 
         @pl.when(core == 1)
         def _():
-            wait_recv(st0_copy(i))
-            guarded(i >= 2, lambda: wait_send(st1_copy(i)))
+            wait_recv(st0_copy(c))
+            guarded(c.n >= 2, lambda: wait_send(st1_copy(c)))
             mid[s, 0:1, :] = join([st0[s, 0:1, :], own[s, 0:1, :]])
             mid[s, 1:2, :] = st0[s, 1:2, :] + own[s, 1:2, :]
-            start(st1_copy(i))
-
-    def st_row(i):
-        s = lax.rem(i, 2)
-        st_wait(st1_copy(i), 0)
+            start(st1_copy(c))
+
+    def st_row(c):
+        s = c.two
+        st_wait(st1_copy(c), 0)
 
         @pl.when(core == 0)
         def _():
-            guarded(i >= 2, lambda: wait_send(st2_copy(i)))
+            guarded(c.n >= 2, lambda: wait_send(st2_copy(c)))
             row[s, 0:1, :] = join([st1[s, k, 0:1, :] for k in range(side)])
             row[s, 1:2, :] = functools.reduce(jnp.add, [st1[s, k, 1:2, :] for k in range(side)])
             st2[s, y] = row[s]
-            start(st2_copy(i))
-
-    def st_all(i):
-        s = lax.rem(i, 2)
-        st_wait(st2_copy(i), 1)
+            start(st2_copy(c))
+
+    def st_all(c):
+        s = c.two
+        st_wait(st2_copy(c), 1)
         full = join([st2[s, k, 0:1, :] for k in range(side)])
         hit = functools.reduce(jnp.add, [st2[s, k, 1:2, :] for k in range(side)])
         lse[0:1, :] = full + math.log2(tokens)
         lossacc[...] += full - hit
 
+    def chunk(i, k):
+        return Chunk(i - k, lax.rem(i + 8 - k, 2), lax.rem(i + 9 - k, 3))
+
     def step(i, carry):
-        c = i - 2
-        slot = lax.rem(i, 2)
-        has_a, has_c = i < chunks, jnp.logical_and(c >= 0, c < chunks)
+        ch = [chunk(i, k) for k in range(6)]
+        has = [jnp.logical_and(c.n >= 0, c.n < chunks) for c in ch]
+        has_a, has_c = has[0], has[2]
+        ch[2].two = ch[0].two
+        calm = jnp.logical_and(i >= 7, i < chunks)
 
         @pl.when(i + 1 < chunks)
         def _():
-            h_start(i + 1)
+            h_start(i + 1, ch[1].two)
+
+        coming = ch[1 + LATE]
+
+        @pl.when(jnp.logical_and(coming.n >= 0, coming.n < chunks))
+        def _():
+            h_start(coming.n, 2 + coming.two)
 
         @pl.when(has_a)
         def _():
-            h_wait(i)
+            h_wait(ch[0].two)
 
         @pl.when(jnp.logical_and(has_a, has_c))
         def _():
-            two(lambda j: (grad_logits(c, j, slot), logits(i, j, slot)))
+            two(lambda j: (grad_logits(ch[2], j), logits(ch[0], j)))
 
         @pl.when(jnp.logical_and(has_a, jnp.logical_not(has_c)))
         def _():
-            two(lambda j: logits(i, j, slot))
-            two(lambda j: statistics(i, j, slot))
+            def first(j):
+                pl.when(jnp.logical_and(i == 0, j == 1))(w_local[1].wait)
+                logits(ch[0], j)
+
+            two(first)
+            two(lambda j: statistics(ch[0], j))
+
+        @pl.when(i == 0)
+        def _():
+            pl.semaphore_wait(barrier, len(friends))
+            w_remote.start()
 
         @pl.when(jnp.logical_and(has_c, jnp.logical_not(has_a)))
         def _():
-            two(lambda j: grad_logits(c, j, slot))
-
-        def live(k):
-            return jnp.logical_and(k >= 0, k < chunks)
-
-        def live(k):
-            return jnp.logical_and(k >= 0, k < chunks)
-
-        calm = jnp.logical_and(i >= 7, i < chunks)
+            two(lambda j: grad_logits(ch[2], j))
 
         def point_a():
-            guarded(has_c, lambda: start(dz_copy(c)))
-            guarded(live(c - 2), lambda: turn(c - 2))
-            guarded(live(c - 1), lambda: start(rs(PURE1, c - 1)))
+            guarded(has_c, lambda: start(dz_copy(ch[2])))
+            guarded(has[4], lambda: turn(ch[4]))
+            guarded(has[3], lambda: start(rs(PURE1, ch[3])))
 
         def point_m():
-            guarded(live(c - 1), lambda: merge1(c - 1))
-            guarded(has_a, lambda: st_own(i))
-            guarded(live(c - 3), lambda: finish(c - 3))
+            guarded(has[3], lambda: merge1(ch[3]))
+            guarded(has_a, lambda: st_own(ch[0]))
+            guarded(has[5], lambda: finish(ch[5]))
 
         def point_b():
-            guarded(live(i - 1), lambda: st_all(i - 1))
-            guarded(has_a, lambda: st_pair(i))
-            guarded(has_c, lambda: (start(rs(FAR1, c)), wait_send(dz_copy(c))))
-            guarded(live(c - 2), lambda: merge2(c - 2))
+            guarded(has[1], lambda: st_all(ch[1]))
+            guarded(has_a, lambda: st_pair(ch[0]))
+            guarded(has_c, lambda: (start(rs(FAR1, ch[2])), wait_send(dz_copy(ch[2]))))
+            guarded(has[4], lambda: merge2(ch[4]))
 
         both_ways(calm, point_a)
 
-        now = jnp.logical_and(c >= 0, c < chunks - 2)
-
-        @pl.when(now)
+        late = ch[2 + LATE]
+        with_statistics = jnp.logical_and(has_a, late.n >= 0)
+
+        @pl.when(jnp.logical_and(late.n >= 0, late.n < chunks - 1))
+        def _():
+            h_wait(2 + late.two)
+
+        @pl.when(with_statistics)
         def _():
             def half_dw(j):
-                statistics(i, j, slot)
-                grad_w(c, j)
+                statistics(ch[0], j)
+                grad_w(late, j)
 
             lax.fori_loop(0, one, lambda j, u: (half_dw(j), u)[1], 0)
-            both_ways(calm, lambda: guarded(live(i - 1), lambda: st_row(i - 1)))
+            both_ways(calm, lambda: guarded(has[1], lambda: st_row(ch[1])))
             lax.fori_loop(one, 2, lambda j, u: (half_dw(j), u)[1], 0)
 
-        pl.when(jnp.logical_and(jnp.logical_not(now), live(i - 1)))(lambda: st_row(i - 1))
-
-        @pl.when(c == chunks)
-        def _():
-            two(lambda j: grad_w(c - 2, j))
+        @pl.when(jnp.logical_not(with_statistics))
+        def _():
+            pl.when(jnp.logical_and(has_a, has_c))(lambda: two(lambda j: statistics(ch[0], j)))
+            pl.when(has[1])(lambda: st_row(ch[1]))
+            pl.when(jnp.logical_and(i >= chunks, i < chunks + 3))(lambda: two(lambda j: grad_w(late, j)))
 
         both_ways(calm, point_m)
 
         @pl.when(has_c)
         def _():
-            pl.when(c == 0)(w_remote.wait_recv)
-            wait_recv(dz_copy(c))
-            grad_h(c)
+            pl.when(i == 2)(w_remote.wait_recv)
+            wait_recv(dz_copy(ch[2]))
+            grad_h(ch[2])
 
         both_ways(calm, point_b)
 
-        @pl.when(c == chunks)
-        def _():
-            two(lambda j: grad_w(c - 1, j))
+        @pl.when(i == chunks + 2)
+        def _():
+            h_wait(2 + coming.two)
+            two(lambda j: grad_w(coming, j))
             pltpu.make_async_copy(dwacc, dw_hbm, dwsem).start()
 
         return carry
@@ -379,8 +389,9 @@
     lax.fori_loop(0, chunks + 5, step, 0)
 
     for i in range(max(chunks - 2, 0), chunks):
-        guarded(core == 0, lambda: wait_send(st0_copy(i) + st2_copy(i)))
-        guarded(core == 1, lambda: wait_send(st1_copy(i)))
+        c = Chunk(i, i % 2, i % 3)
+        guarded(core == 0, lambda: wait_send(st0_copy(c) + st2_copy(c)))
+        guarded(core == 1, lambda: wait_send(st1_copy(c)))
         pltpu.make_async_copy(ob.at[i % 2], dh_hbm.at[i], osem.at[i % 2]).wait()
     w_remote.wait_send()
     pltpu.make_async_copy(dwacc, dw_hbm, dwsem).wait()
@@ -435,7 +446,7 @@
                 pltpu.VMEM((vocab, dim), F32),
                 pltpu.VMEM((4, 2 * side, side, ROWS, dim), BF16),
                 pltpu.VMEM((2, vocab, tok), F32),
-                pltpu.VMEM((2, 2, vocab, tok // 2), BF16),
+                pltpu.VMEM((3, 2, vocab, tok // 2), BF16),
                 pltpu.VMEM((2, vocab, tok // 2), BF16),
                 pltpu.VMEM((2, side, side * ROWS, dim), F32),
                 pltpu.VMEM((2, side, ROWS, dim), F32),
@@ -451,7 +462,7 @@
                 pltpu.VMEM((2, side, 2, tok), F32),
                 pltpu.VMEM((1, tok), F32),
                 pltpu.VMEM((1, tok), F32),
-                dma, dma((4,)),
+                dma((2,)), dma((4,)),
                 dma((6, 3, 2)), dma((6, 3, 2)),
                 dma, dma((2,)), dma, dma,
                 dma((2,)), dma((2,)),

time: 440 us -> 441 us (level)
  no operation moved by 1% of the time
where the time goes in v4:
time: 441 us
  Pallas kernels  436 us (99%)
    pallas_call x1, Pallas kernels, local_step(): pl.pallas_call(functools.partial(head_kernel, group, side, chunks, tokens...  424 us
    pallas_call x1, Pallas kernels, local_step(): pl.pallas_call(copy_kernel, out_shape=(jax.ShapeDtypeStruct((vocab, dim),...  12 us

profile of v4, /device:TPU:96, one launch (start us, length us, event | category | flops | bytes accessed | tf_op | source)
XLA Modules:
  0.0 440.7 jit_solution(15528887688133308553)
XLA Ops:
  0.6 1.0 reshape.22
  1.7 0.1 copy.7
  1.8 0.1 copy.9
  1.9 0.1 copy.8
  2.0 0.1 copy.10
  2.1 0.7 pad_add_fusion.tgt
  2.8 424.2 %head.1 = (f32[1,128]{1,0:T(1,128)}, f32[32,16,2048]{2,1,0:T(8,128)}, f32[1536,2048]{1,0:T(8,128)}) custom-call(bf16[4,4,2,32,16,2048]{5,4,3,2,1,0:T(8,128)(2,1)} %bitcast.hid, s32[32,1,512]{2,1,0:T(1,128)} %pad_add_fusion.tgt, bf16[1536,2048]{1,0:T(8,128)(2,1)} %w_hbm.1), custom_call_target="tpu_custom_call" | custom-call | tf_op jit(solution)/shard_map/head/pallas_call | solution.py:435
  427.0 12.0 %results.1 = (f32[1536,2048]{1,0:T(8,128)}, f32[512,2048]{1,0:T(8,128)}) custom-call(f32[1536,2048]{1,0:T(8,128)} %get-tuple-element.9.dw_hbm, f32[512,2048]{1,0:T(8,128)} %bitcast.14), custom_call_target="tpu_custom_call" | custom-call | tf_op jit(solution)/shard_map/results/pallas_call | solution.py:480
  (1 shorter events, 0.0 us)

commit v5 on v3

--- a/solution.py
+++ b/solution.py
@@ -184,9 +184,11 @@
 
     def grad_logits(c, j, slot):
         r = pl.ds(pl.multiple_of(j * mt, mt), mt)
-        prob = jnp.exp2(yb[slot, r, :] - lse[0:1, :])
-        hit = lax.broadcasted_iota(jnp.int32, prob.shape, 0) == tgt[c] - (me * vocab + j * mt)
-        g = (prob + jnp.where(hit, -1.0 / tokens, 0.0)).astype(BF16)
+        prob = jnp.exp2(yb[slot, r, :] - lse[0:1, :]).astype(BF16)
+        at_hit = (jnp.exp2(own[slot, 1:2, :] - lse[0:1, :]) - 1.0 / tokens).astype(BF16)
+        rel = jnp.clip(tgt[c] - (me * vocab + j * mt), -1, mt).astype(jnp.int16)
+        hit = lax.broadcasted_iota(jnp.int32, prob.shape, 0).astype(jnp.int16) == rel
+        g = jnp.where(hit, at_hit, prob)
         dz[slot, 0, r, :] = g[:, :tokc]
         dz[slot, 1, r, :] = g[:, tokc:]
 
@@ -304,7 +306,9 @@
 
         @pl.when(jnp.logical_and(has_a, has_c))
         def _():
-            two(lambda j: (grad_logits(c, j, slot), logits(i, j, slot)))
+            for j in range(2):
+                grad_logits(c, j, slot)
+                logits(i, j, slot)
 
         @pl.when(jnp.logical_and(has_a, jnp.logical_not(has_c)))
         def _():

time: 440 us -> 430 us (0.977)
  Pallas kernels: 435 us -> 425 us
    pallas_call x1, Pallas kernels: 423 us -> 413 us  [local_step(): pl.pallas_call(functools.partial(head_kernel, group, side, chunks, tokens...]
where the time goes in v5:
time: 430 us
  Pallas kernels  425 us (99%)
    pallas_call x1, Pallas kernels, local_step(): pl.pallas_call(functools.partial(head_kernel, group, side, chunks, tokens...  413 us
    pallas_call x1, Pallas kernels, local_step(): pl.pallas_call(copy_kernel, out_shape=(jax.ShapeDtypeStruct((vocab, dim),...  12 us

profile of v5, /device:TPU:96, one launch (start us, length us, event | category | flops | bytes accessed | tf_op | source)
XLA Modules:
  0.0 429.9 jit_solution(3791794747078046455)
XLA Ops:
  0.6 1.0 reshape.22
  1.7 0.1 copy.7
  1.8 0.1 copy.9
  1.9 0.1 copy.8
  2.0 0.1 copy.10
  2.1 0.7 pad_add_fusion.tgt
  2.8 413.3 %head.1 = (f32[1,128]{1,0:T(1,128)}, f32[32,16,2048]{2,1,0:T(8,128)}, f32[1536,2048]{1,0:T(8,128)}) custom-call(bf16[4,4,2,32,16,2048]{5,4,3,2,1,0:T(8,128)(2,1)} %bitcast.hid, s32[32,1,512]{2,1,0:T(1,128)} %pad_add_fusion.tgt, bf16[1536,2048]{1,0:T(8,128)(2,1)} %w_hbm.1), custom_call_target="tpu_custom_call" | custom-call | tf_op jit(solution)/shard_map/head/pallas_call | solution.py:428
  416.1 12.0 %results.1 = (f32[1536,2048]{1,0:T(8,128)}, f32[512,2048]{1,0:T(8,128)}) custom-call(f32[1536,2048]{1,0:T(8,128)} %get-tuple-element.9.dw_hbm, f32[512,2048]{1,0:T(8,128)} %bitcast.14), custom_call_target="tpu_custom_call" | custom-call | tf_op jit(solution)/shard_map/results/pallas_call | solution.py:473
  (1 shorter events, 0.0 us)

commit v6 on v5

--- a/solution.py
+++ b/solution.py
@@ -38,7 +38,7 @@
 
 def head_kernel(
     group, side, chunks, tokens,
-    hid, tgt, w_hbm,
+    hid, tgt0, tgt1, w_hbm,
     loss_ref, dh_hbm, dw_hbm,
     wb, dwacc, hb, yb, dz, dzr, sb, tb, far1, pure1, merged1, far2, pure2, merged2, ob,
     stat, own, st0, mid, st1, row, st2, lse, lossacc,
@@ -177,16 +177,19 @@
     def two(fn):
         lax.fori_loop(0, 2, lambda j, carry: (fn(j), carry)[1], 0)
 
-    def logits(i, j, slot):
+    def targets(n):
+        return jnp.concatenate([tgt0[n], tgt1[n]], axis=1)
+
+    def logits(i, j, slot, mt=mt):
         r = pl.ds(pl.multiple_of(j * mt, mt), mt)
         h = hb[lax.rem(i, 4)].reshape(tok, dim)
         yb[slot, r, :] = dot_nt(wb[core, r, :], h) * LOG2E
 
-    def grad_logits(c, j, slot):
+    def grad_logits(c, j, slot, mt=mt):
         r = pl.ds(pl.multiple_of(j * mt, mt), mt)
         prob = jnp.exp2(yb[slot, r, :] - lse[0:1, :]).astype(BF16)
         at_hit = (jnp.exp2(own[slot, 1:2, :] - lse[0:1, :]) - 1.0 / tokens).astype(BF16)
-        rel = jnp.clip(tgt[c] - (me * vocab + j * mt), -1, mt).astype(jnp.int16)
+        rel = jnp.clip(targets(c) - (me * vocab + j * mt), -1, mt).astype(jnp.int16)
         hit = lax.broadcasted_iota(jnp.int32, prob.shape, 0).astype(jnp.int16) == rel
         g = jnp.where(hit, at_hit, prob)
         dz[slot, 0, r, :] = g[:, :tokc]
@@ -196,7 +199,7 @@
         v = yb[slot, pl.ds(pl.multiple_of(j * mt, mt), mt), :]
         top = jnp.max(v, axis=0, keepdims=True)
         total = jnp.sum(jnp.exp2(v - top), axis=0, keepdims=True)
-        hit = lax.broadcasted_iota(jnp.int32, v.shape, 0) == tgt[lax.rem(i, chunks)] - (me * vocab + j * mt)
+        hit = lax.broadcasted_iota(jnp.int32, v.shape, 0) == targets(lax.rem(i, chunks)) - (me * vocab + j * mt)
         stat[j, 0:1, :] = top + jnp.log(total) * LOG2E
         stat[j, 1:2, :] = jnp.sum(jnp.where(hit, v, 0.0), axis=0, keepdims=True)
 
@@ -229,7 +232,6 @@
         hi = sb[s, p, :, half:] + pure1[s, 0] + merged1[s, 1]
         tb[s, :, :, :half] = lo.reshape(side, ROWS, half)
         tb[s, :, :, half:] = hi.reshape(side, ROWS, half)
-        start(rs(FAR2, c) + rs(PURE2, c))
         wait_send(rs(FAR1, c) + rs(PURE1, c) + rs(MERGED1, c))
 
     def merge1(c):
@@ -306,14 +308,16 @@
 
         @pl.when(jnp.logical_and(has_a, has_c))
         def _():
+            for j in range(4):
+                grad_logits(c, j, slot, vocab // 4)
+                logits(i, j, slot, vocab // 4)
+
+        @pl.when(jnp.logical_and(has_a, jnp.logical_not(has_c)))
+        def _():
             for j in range(2):
-                grad_logits(c, j, slot)
                 logits(i, j, slot)
-
-        @pl.when(jnp.logical_and(has_a, jnp.logical_not(has_c)))
-        def _():
-            two(lambda j: logits(i, j, slot))
-            two(lambda j: statistics(i, j, slot))
+            for j in range(2):
+                statistics(i, j, slot)
 
         @pl.when(jnp.logical_and(has_c, jnp.logical_not(has_a)))
         def _():
@@ -331,6 +335,10 @@
             guarded(has_c, lambda: start(dz_copy(c)))
             guarded(live(c - 2), lambda: turn(c - 2))
             guarded(live(c - 1), lambda: start(rs(PURE1, c - 1)))
+
+        def point_r():
+            guarded(live(i - 1), lambda: st_row(i - 1))
+            guarded(live(c - 2), lambda: start(rs(FAR2, c - 2) + rs(PURE2, c - 2)))
 
         def point_m():
             guarded(live(c - 1), lambda: merge1(c - 1))
@@ -354,10 +362,10 @@
                 grad_w(c, j)
 
             lax.fori_loop(0, one, lambda j, u: (half_dw(j), u)[1], 0)
-            both_ways(calm, lambda: guarded(live(i - 1), lambda: st_row(i - 1)))
+            both_ways(calm, point_r)
             lax.fori_loop(one, 2, lambda j, u: (half_dw(j), u)[1], 0)
 
-        pl.when(jnp.logical_and(jnp.logical_not(now), live(i - 1)))(lambda: st_row(i - 1))
+        pl.when(jnp.logical_not(now))(point_r)
 
         @pl.when(c == chunks)
         def _():
@@ -417,10 +425,8 @@
         half = dim // 2
         hid = hidden.reshape(side, side, 2, chunks, ROWS, dim)
         t = targets.reshape(side, side, 2, chunks, ROWS)
-        tgt = jnp.concatenate(
-            [t[:, :, 0].transpose(2, 1, 0, 3).reshape(chunks, 1, tok // 2), t[:, :, 1].transpose(2, 0, 1, 3).reshape(chunks, 1, tok // 2)],
-            axis=2,
-        )
+        tgt0 = t[:, :, 0].transpose(2, 1, 0, 3).reshape(chunks, 1, tok // 2)
+        tgt1 = t[:, :, 1].transpose(2, 0, 1, 3).reshape(chunks, 1, tok // 2)
         dma = pltpu.SemaphoreType.DMA
         any_spec = pl.BlockSpec(memory_space=pl.ANY)
         vmem_spec = pl.BlockSpec(memory_space=pltpu.VMEM)
@@ -432,7 +438,7 @@
                 jax.ShapeDtypeStruct((chunks, ROWS, dim), F32),
                 jax.ShapeDtypeStruct((vocab, dim), F32),
             ),
-            in_specs=[any_spec, vmem_spec, any_spec],
+            in_specs=[any_spec, vmem_spec, vmem_spec, any_spec],
             out_specs=(vmem_spec, any_spec, any_spec),
             scratch_shapes=[
                 pltpu.VMEM((2, vocab, dim), BF16),
@@ -467,7 +473,7 @@
                 collective_id=0, has_side_effects=True, vmem_limit_bytes=67043328,
             ),
             name="head",
-        )(hid, tgt, w_blk)
+        )(hid, tgt0, tgt1, w_blk)
         rows = tokens // group // 4
         pieces = (vocab + tokens // group) // rows
         dw, dh = pl.pallas_call(

time: 430 us -> 430 us (level)
  no operation moved by 1% of the time
where the time goes in v6:
time: 430 us
  Pallas kernels  425 us (99%)
    pallas_call x1, Pallas kernels, local_step(): pl.pallas_call(functools.partial(head_kernel, group, side, chunks, tokens...  413 us
    pallas_call x1, Pallas kernels, local_step(): pl.pallas_call(copy_kernel, out_shape=(jax.ShapeDtypeStruct((vocab, dim),...  12 us

profile of v6, /device:TPU:96, one launch (start us, length us, event | category | flops | bytes accessed | tf_op | source)
XLA Modules:
  0.0 429.9 jit_solution(15330047616191168191)
XLA Ops:
  0.6 1.0 reshape.22
  1.7 0.1 copy.8
  1.8 0.7 copy.10.tgt1
  2.5 0.1 copy.7
  2.6 0.7 copy.9.tgt0
  3.3 412.8 %head.1 = (f32[1,128]{1,0:T(1,128)}, f32[32,16,2048]{2,1,0:T(8,128)}, f32[1536,2048]{1,0:T(8,128)}) custom-call(bf16[4,4,2,32,16,2048]{5,4,3,2,1,0:T(8,128)(2,1)} %bitcast.hid, s32[32,1,256]{2,1,0:T(1,128)} %copy.9.tgt0, s32[32,1,256]{2,1,0:T(1,128)} %copy.10.tgt1, bf16[1536,2048]{1,0:T(8,128)(2,1)} %w_hbm.1), custom_call_target="tpu_custom_call" | custom-call | tf_op jit(solution)/shard_map/head/pallas_call | solution.py:434
  416.1 12.0 %results.1 = (f32[1536,2048]{1,0:T(8,128)}, f32[512,2048]{1,0:T(8,128)}) custom-call(f32[1536,2048]{1,0:T(8,128)} %get-tuple-element.9.dw_hbm, f32[512,2048]{1,0:T(8,128)} %bitcast.14), custom_call_target="tpu_custom_call" | custom-call | tf_op jit(solution)/shard_map/results/pallas_call | solution.py:479
  (1 shorter events, 0.0 us)
